TPU v7x, 32 devices: a whole 2x2x4 slice. The times are simulated.
32 devices in a mesh: row: 8 (over z, y), col: 4 (over x, core).
Axes of the slice: x: 2, y: 2, z: 4, core: 2. Of those that a mesh axis runs over, the one named last changes fastest.
Arguments:
- amplitudes: float32 [128, 512, 512], P(('row', 'col')), may hold values from -6 to 6
- integrals: float32 [512, 1024, 1024], P(('row', 'col')), may hold values from -0.01171875 to 0.01171875
- coupling: float32 [512, 32, 1024], P(('row', 'col')), may hold values from -0.046875 to 0.046875
- task_table: int32 [32, 16, 2], replicated, may hold values from -1 to 15, as said below
Outputs:
- residual: float32 [128, 1024], P(('row', 'col'))
Inputs may be any that keep to these rules, and one draw needn't show every extreme that they name: `task_table`: every virtual tile pair (C, D), C and D in 0 to 15, appears in exactly one slot. In each device's row the valid slots come first and the rest hold -1 in both entries. Some device has all 16 slots valid and some device has none. `integrals`: slots that task_table marks -1 are not read.
All inputs are finite; a program needn't handle non-finite values.
Results may differ from a plain program's by a relative error of at most 0.0003.
Values sent between devices are 32-bit elements; how exact they have to be, the bound alone decides.
A program may use at most 192 MiB of HBM per device.

v0:
```python
import functools

import jax
import jax.numpy as jnp
from jax import lax
from jax.experimental import pallas as pl
from jax.experimental.pallas import tpu as pltpu
from jax.sharding import PartitionSpec as P

TB = 32
NVT = 16
LANES = 128
GROUP = LANES // TB
SUB = TB * TB // LANES


def pack_kernel(local_rows, slots_all, ids_ref, amp_ref, out_ref, held, sems):
    wide = NVT * TB
    copies = []
    for h in range(wide // LANES):
        for r in range(local_rows):
            n = h * local_rows + r
            copies.append(
                pltpu.make_async_copy(
                    amp_ref.at[r, :, pl.ds(h * LANES, LANES)],
                    held.at[pl.ds(n * wide, wide), :],
                    sems.at[n],
                )
            )
    for copy in copies:
        copy.start()
    for copy in copies:
        copy.wait()
    chunk = lax.broadcasted_iota(jnp.int32, (SUB, LANES), 1) // TB

    def one_slot(k, carry):
        pair = ids_ref[k]

        @pl.when(pair >= 0)
        def _():
            upper = pair // NVT
            lower = pair % NVT
            h = lower // GROUP
            low = lower % GROUP
            for r in range(local_rows):
                base = (h * local_rows + r) * wide + upper * TB
                value = jnp.zeros((SUB, LANES), jnp.float32)
                for j in range(GROUP):
                    x = held[pl.ds(base + j, SUB, stride=GROUP), :]
                    x = pltpu.roll(x, ((j - low + GROUP) % GROUP) * TB, 1)
                    value = jnp.where(chunk == j, x, value)
                out_ref[k, pl.ds(r * SUB, SUB), :] = value

        return carry

    lax.fori_loop(0, slots_all, one_slot, 0)


def pack(amplitudes, ids, slots_all):
    local_rows = amplitudes.shape[0]
    groups = NVT * TB // LANES
    return pl.pallas_call(
        functools.partial(pack_kernel, local_rows, slots_all),
        out_shape=jax.ShapeDtypeStruct((slots_all, local_rows * SUB, LANES), jnp.float32),
        in_specs=[
            pl.BlockSpec(memory_space=pltpu.SMEM),
            pl.BlockSpec(memory_space=pl.ANY),
        ],
        out_specs=pl.BlockSpec(memory_space=pltpu.VMEM),
        scratch_shapes=[
            pltpu.VMEM((groups * local_rows * NVT * TB, LANES), jnp.float32),
            pltpu.SemaphoreType.DMA((groups * local_rows,)),
        ],
        compiler_params=pltpu.CompilerParams(vmem_limit_bytes=32 * 1024 * 1024),
        name="pack",
    )(ids, amplitudes)


def ladder_kernel(rows, count_ref, a_ref, v_ref, out_ref, flat, both, total):
    s = pl.program_id(0)

    @pl.when(s == 0)
    def _():
        total[...] = jnp.zeros_like(total)

    @pl.when(s < count_ref[0])
    def _():
        flat[...] = a_ref[:, 0].reshape(rows * SUB, LANES)
        for k in range(SUB):
            a = flat[pl.ds(k, rows, stride=SUB), :]
            high = a.astype(jnp.bfloat16)
            low = (a - high.astype(jnp.float32)).astype(jnp.bfloat16)
            both[pl.ds(0, rows), pl.ds(k * LANES, LANES)] = high
            both[pl.ds(rows, rows), pl.ds(k * LANES, LANES)] = low
        dims = (((1,), (1,)), ((), ()))
        step = 256
        for i in range(TB * TB // step):
            part = pl.ds(i * step, step)
            v = v_ref[0, part, :]
            vh = v.astype(jnp.bfloat16)
            vl = (v - vh.astype(jnp.float32)).astype(jnp.bfloat16)
            b = both[...]
            total[part, :] += lax.dot_general(
                vh, b, dims, preferred_element_type=jnp.float32
            ) + lax.dot_general(vl, b, dims, preferred_element_type=jnp.float32)

    @pl.when(s == pl.num_programs(0) - 1)
    def _():
        out_ref[...] = (total[:, :rows] + total[:, rows:]).T


def ladder_of(arrived, integrals, count):
    devices_all, slot_total, depth, _ = arrived.shape
    rows = devices_all * depth // SUB
    size = TB * TB

    def at(s, count_ref):
        return jnp.minimum(s, jnp.maximum(count_ref[0] - 1, 0))

    return pl.pallas_call(
        functools.partial(ladder_kernel, rows),
        out_shape=jax.ShapeDtypeStruct((rows, size), jnp.float32),
        grid_spec=pltpu.PrefetchScalarGridSpec(
            num_scalar_prefetch=1,
            grid=(slot_total,),
            in_specs=[
                pl.BlockSpec((devices_all, 1, depth, LANES), lambda s, c: (0, at(s, c), 0, 0)),
                pl.BlockSpec((1, size, size), lambda s, c: (at(s, c), 0, 0)),
            ],
            out_specs=pl.BlockSpec((rows, size), lambda s, c: (0, 0)),
            scratch_shapes=[
                pltpu.VMEM((rows * SUB, LANES), jnp.float32),
                pltpu.VMEM((2 * rows, size), jnp.bfloat16),
                pltpu.VMEM((size, 2 * rows), jnp.float32),
            ],
        ),
        compiler_params=pltpu.CompilerParams(
            dimension_semantics=("arbitrary",), vmem_limit_bytes=32 * 1024 * 1024
        ),
        name="ladder",
    )(count, arrived, integrals)


def body(amplitudes, integrals, coupling, task_table):
    devices_all = lax.axis_size("row") * lax.axis_size("col")
    local_rows = amplitudes.shape[0]
    slot_total = integrals.shape[0]
    total_rows = devices_all * local_rows
    upper, lower = task_table[:, :, 0], task_table[:, :, 1]
    ids = jnp.where(upper >= 0, upper * NVT + lower, -1)

    first_tile = amplitudes[:, :TB, :]
    pieces = lax.all_to_all(first_tile, ("row", "col"), split_axis=2, concat_axis=0, tiled=True)
    outgoing = pack(amplitudes, ids.reshape(-1), devices_all * slot_total).reshape(
        devices_all, slot_total * local_rows * SUB, LANES
    )
    arrived = lax.all_to_all(outgoing, ("row", "col"), split_axis=0, concat_axis=0, tiled=True)
    arrived = arrived.reshape(devices_all, slot_total, local_rows * SUB, LANES)

    own_index = lax.axis_index(("row", "col"))
    own_ids = lax.dynamic_index_in_dim(ids, own_index, 0, keepdims=False)
    count = jnp.sum((own_ids >= 0).astype(jnp.int32)).reshape(1)
    ladder = ladder_of(arrived, integrals, count)

    width_part = pieces.shape[2]
    occupied = coupling.shape[1]
    window = total_rows // occupied
    regrouped = jnp.transpose(
        pieces.reshape(window, occupied, TB, width_part), (0, 2, 3, 1)
    ).reshape(window * TB, width_part * occupied)
    coupling_rows = coupling.reshape(width_part * occupied, occupied * TB)
    hole_term = jnp.dot(
        regrouped,
        coupling_rows,
        precision=lax.Precision.HIGHEST,
        preferred_element_type=jnp.float32,
    )
    hole_term = jnp.transpose(hole_term.reshape(window, TB, occupied, TB), (0, 2, 1, 3)).reshape(
        total_rows, TB * TB
    )
    partial = (ladder + hole_term).reshape(devices_all, local_rows * SUB, LANES)
    shares = lax.all_to_all(partial, ("row", "col"), split_axis=0, concat_axis=0, tiled=True)
    return jnp.sum(shares, axis=0).reshape(local_rows, TB * TB)


def solution(mesh):
    in_specs = (
        P(("row", "col"), None, None),
        P(("row", "col"), None, None),
        P(("row", "col"), None, None),
        P(),
    )
    out_specs = P(("row", "col"), None)
    return jax.shard_map(body, mesh=mesh, in_specs=in_specs, out_specs=out_specs, check_vma=False)
```

profile of v0, /device:TPU:0, one launch (start us, length us, event | category | flops | bytes accessed | tf_op | source)
XLA Modules:
  0.0 283.6 jit_solution(4547583531414929704)
XLA Ops:
  0.0 1.0 slice.11
  1.0 0.4 copy.12
  1.4 1.4 reshape.65
  2.8 7.3 %all-to-all-start.1 = ((f32[32,1,2048]{2,1,0:T(1,128)}), f32[32,1,2048]{2,1,0:T(1,128)S(1)}, u32[]{:S(2)}, u32[]{:S(2)}) async-start(f32[32,1,2048]{2,1,0:T(1,128)} %reshape.65), calls=%async_computation.1 | async-start | bytes 524288 | tf_op jit(solution)/shard_map/all_to_all | solution.py:153
  10.2 0.1 select_n.15.ids_ref
  10.3 2.2 copy-done.1
  12.5 26.0 %pack.1 = f32[512,32,128]{2,1,0:T(8,128)S(1)} custom-call(s32[512]{0:T(512)S(1)} %select_n.15.ids_ref, f32[4,512,512]{2,1,0:T(8,128)S(1)} %copy-done.1), custom_call_target="tpu_custom_call" | custom-call | tf_op jit(solution)/shard_map/pack/pallas_call | solution.py:62
  38.5 3.2 %copy-done = f32[512,32,128]{2,1,0:T(8,128)} copy-done((f32[512,32,128]{2,1,0:T(8,128)}, f32[512,32,128]{2,1,0:T(8,128)S(1)}, u32[]{:S(2)}) %copy-start) | copy-done | bytes 8388632
  41.7 6.0 %all-to-all-start = ((f32[32,512,128]{2,1,0:T(8,128)}), f32[32,512,128]{2,1,0:T(8,128)}, u32[]{:S(2)}, u32[]{:S(2)}) async-start(f32[32,512,128]{2,1,0:T(8,128)} %bitcast.29), calls=%async_computation | async-start | bytes 16777216 | tf_op jit(solution)/shard_map/all_to_all | solution.py:157
  47.7 1.9 copy.16
  49.6 0.7 fusion.1
  50.3 0.5 broadcast.24
  50.8 1.2 reduce.2
  52.1 0.5 reshape.66
  52.7 0.1 copy.14
  52.8 0.7 copy.15
  53.5 0.4 reshape.62
  54.0 6.4 %convolution_bitcast_fusion = f32[4,32,32,32]{3,2,1,0:T(8,128)S(1)} fusion(f32[32,32,512,1]{2,1,0,3:T(8,128)} %bitcast.30, f32[4,32,512,1]{2,1,0,3:T(8,128)S(1)} %reshape.62), kind=kOutput, calls=%fused_computation | convolution fusion | flops 805306368 | bytes 2883584 | tf_op jit(solution)/shard_map/dot_general | solution.py:172
  60.4 1.0 reshape.58
  61.3 172.3 %all-to-all-done = f32[32,512,128]{2,1,0:T(8,128)} async-done(((f32[32,512,128]{2,1,0:T(8,128)}), f32[32,512,128]{2,1,0:T(8,128)}, u32[]{:S(2)}, u32[]{:S(2)}) %all-to-all-start) | async-done | bytes 8388640 | tf_op jit(solution)/shard_map/all_to_all | solution.py:157
  233.6 24.6 %ladder.1 = f32[128,1024]{1,0:T(8,128)S(1)} custom-call(s32[1]{0:T(128)} %bitcast.count_ref, f32[32,16,32,128]{3,2,1,0:T(8,128)} %bitcast.2.a_ref, f32[16,1024,1024]{2,1,0:T(8,128)} %v_ref.1), custom_call_target="tpu_custom_call" | custom-call | tf_op jit(solution)/shard_map/ladder/pallas_call | solution.py:120
  258.3 0.1 reshape.59
  258.4 24.6 %all_to_all.25 = f32[32,32,128]{2,1,0:T(8,128)S(1)} all-to-all(f32[32,32,128]{2,1,0:T(8,128)S(1)} %reshape.59), channel_id=1, replica_groups=mesh['row'=8,'col'=4] {'row','col'}, dimensions={0} | all-to-all | bytes 1048576 | tf_op jit(solution)/shard_map/all_to_all | solution.py:182
  283.0 0.6 reshape.60
  (12 shorter events, 0.3 us)
Async XLA Ops:
  0.0 10.1 %copy-start.3 = (s32[32,16,2]{0,2,1:T(2,128)S(1)}, s32[32,16,2]{0,2,1:T(2,128)}, u32[]{:S(2)}) copy-start(s32[32,16,2]{0,2,1:T(2,128)} %param.7) | copy-start | bytes 12292
  2.8 39.0 %all-to-all-start.1 = ((f32[32,1,2048]{2,1,0:T(1,128)}), f32[32,1,2048]{2,1,0:T(1,128)S(1)}, u32[]{:S(2)}, u32[]{:S(2)}) async-start(f32[32,1,2048]{2,1,0:T(1,128)} %reshape.65), calls=%async_computation.1 | async-start | bytes 524288 | tf_op jit(solution)/shard_map/all_to_all | solution.py:153
  10.3 2.2 copy-start.1
  38.5 3.2 %copy-start = (f32[512,32,128]{2,1,0:T(8,128)}, f32[512,32,128]{2,1,0:T(8,128)S(1)}, u32[]{:S(2)}) copy-start(f32[512,32,128]{2,1,0:T(8,128)S(1)} %pack.1) | copy-start | bytes 25165828
  41.7 6.0 %copy-start.2 = (f32[16,32,1024]{2,1,0:T(8,128)S(1)}, f32[16,32,1024]{2,1,0:T(8,128)}, u32[]{:S(2)}) copy-start(f32[16,32,1024]{2,1,0:T(8,128)} %param.6) | copy-start | bytes 6291460
  41.7 191.9 %all-to-all-start = ((f32[32,512,128]{2,1,0:T(8,128)}), f32[32,512,128]{2,1,0:T(8,128)}, u32[]{:S(2)}, u32[]{:S(2)}) async-start(f32[32,512,128]{2,1,0:T(8,128)} %bitcast.29), calls=%async_computation | async-start | bytes 16777216 | tf_op jit(solution)/shard_map/all_to_all | solution.py:157
where the time goes:
time: 285 us; the launch traced here: 284 us
  waiting for transfers between devices  172 us (60%)
  Pallas kernels  50.6 us (18%)
  blocking collectives  24.6 us (9%)
  local copies, waits for them, and re-layouts  14.2 us (5%)
  starting transfers between devices  13.3 us (5%)
  matrix products  6.4 us (2%)
    all_to_all x1, waiting for transfers between devices, body(): lax.all_to_all(outgoing, ('row', 'col'), split_axis=0, concat_axis=0, til...  172 us
    pallas_call x1, Pallas kernels, pack(): pl.pallas_call(functools.partial(pack_kernel, local_rows, slots_all), out...  26 us
    pallas_call x1, Pallas kernels, ladder_of(): pl.pallas_call(functools.partial(ladder_kernel, rows), out_shape=jax.Shap...  24.6 us
    all_to_all x1, blocking collectives, body(): lax.all_to_all(partial, ('row', 'col'), split_axis=0, concat_axis=0, tile...  24.6 us
    all_to_all x1, starting transfers between devices, body(): lax.all_to_all(first_tile, ('row', 'col'), split_axis=2, concat_axis=0, t...  7.33 us
    unnamed x10, local copies, waits for them, and re-layouts  7.32 us
    dot_general x1, matrix products, body(): jnp.dot(regrouped, coupling_rows, precision=lax.Precision.HIGHEST, prefer...  6.4 us
    all_to_all x1, starting transfers between devices, body(): lax.all_to_all(outgoing, ('row', 'col'), split_axis=0, concat_axis=0, til...  5.96 us
  transfers between devices with their start and end apart: 2, of which 1 were waited for; matrix products, arithmetic and copies ran while one was open for 5% of the time, Pallas kernels for 9%

commit v1 on v0

v1 whole, which is shorter than its diff:
```python
import functools

import jax
import jax.numpy as jnp
from jax import lax
from jax.experimental import pallas as pl
from jax.experimental.pallas import tpu as pltpu
from jax.sharding import PartitionSpec as P

TB = 32
LANES = 128
GROUP = LANES // TB
SUB = TB * TB // LANES
MESH = pl.DeviceIdType.MESH


def chunk_transpose(x, chunk):
    a0 = jnp.where(chunk < 2, x[0], pltpu.roll(x[2], 2 * TB, 1))
    a2 = jnp.where(chunk < 2, pltpu.roll(x[0], 2 * TB, 1), x[2])
    a1 = jnp.where(chunk < 2, x[1], pltpu.roll(x[3], 2 * TB, 1))
    a3 = jnp.where(chunk < 2, pltpu.roll(x[1], 2 * TB, 1), x[3])
    even = chunk % 2 == 0
    y0 = jnp.where(even, a0, pltpu.roll(a1, TB, 1))
    y1 = jnp.where(even, pltpu.roll(a0, LANES - TB, 1), a1)
    y2 = jnp.where(even, a2, pltpu.roll(a3, TB, 1))
    y3 = jnp.where(even, pltpu.roll(a2, LANES - TB, 1), a3)
    return y0, y1, y2, y3


def exchange_kernel(
    cfg, list_ref, relay_ref, amp_ref, v_ref, out_ref,
    held, packed, send1, land, acc, stage, got, vbuf, flat, both, total,
    amp_sems, s1_send, s1_recv, s2_send, s2_recv, v_sems,
):
    planes, inner, ncol, local, slots, chunks, ct, cap_max, nvt = cfg
    members = inner * ncol
    wide = nvt * TB
    quads = wide // LANES
    depth = planes * local
    rows = members * depth
    per_chunk = slots // chunks
    row = lax.axis_index("row")
    col = lax.axis_index("col")
    z = row // inner
    me = (row % inner) * ncol + col

    copies = []
    for h in range(quads):
        for r in range(local):
            n = h * local + r
            copies.append(
                pltpu.make_async_copy(
                    amp_ref.at[r, :, pl.ds(h * LANES, LANES)],
                    held.at[pl.ds(n * wide, wide), :],
                    amp_sems.at[n],
                )
            )
    for copy in copies:
        copy.start()

    def fetch(t):
        return pltpu.make_async_copy(v_ref.at[slots - 1 - t], vbuf.at[t % 2], v_sems.at[t % 2])

    fetch(0).start()
    fetch(1).start()

    barrier = pltpu.get_barrier_semaphore()
    for d in range(1, planes):
        other = ((z + d) % planes) * inner + row % inner
        pl.semaphore_signal(barrier, inc=1, device_id=(other, col), device_id_type=MESH)
    for d in range(1, members):
        m = (me + d) % members
        pl.semaphore_signal(
            barrier, inc=1, device_id=(z * inner + m // ncol, m % ncol), device_id_type=MESH
        )

    total[...] = jnp.zeros_like(total)
    acc[0] = jnp.zeros(acc.shape[1:], jnp.float32)
    for copy in copies:
        copy.wait()

    lane_chunk = lax.broadcasted_iota(jnp.int32, (SUB, LANES), 1) // TB

    def pack_tile(upper, carry):
        for h in range(quads):
            for r in range(local):
                base = (h * local + r) * wide + upper * TB
                x = [held[pl.ds(base + j, SUB, stride=GROUP), :] for j in range(GROUP)]
                y = chunk_transpose(x, lane_chunk)
                for low in range(GROUP):
                    packed[upper * nvt + h * GROUP + low, r] = y[low]
        return carry

    lax.fori_loop(0, nvt, pack_tile, 0)

    def fill(k, carry):
        def one(t, c):
            for d in range(1, planes):
                tile = list_ref[((z + d) % planes) * cap_max + k * ct + t]
                send1[k, d - 1, t] = packed[tile]
            tile = list_ref[z * cap_max + k * ct + t]
            acc[1 + k * ct + t, pl.ds(z * local, local)] = packed[tile]
            return c

        return lax.fori_loop(0, ct, one, carry)

    def hop1(k, d):
        other = ((z + d) % planes) * inner + row % inner
        return pltpu.make_async_remote_copy(
            src_ref=send1.at[k, d - 1],
            dst_ref=land.at[k, d - 1],
            send_sem=s1_send.at[k, d - 1],
            recv_sem=s1_recv.at[k, d - 1],
            device_id=(other, col),
            device_id_type=MESH,
        )

    def hop2(r, d):
        m = (me + d) % members
        return pltpu.make_async_remote_copy(
            src_ref=stage.at[r, m],
            dst_ref=got.at[r, me],
            send_sem=s2_send.at[r, d - 1],
            recv_sem=s2_recv.at[r, d - 1],
            device_id=(z * inner + m // ncol, m % ncol),
            device_id_type=MESH,
        )

    def got_from(r, d):
        m = (me + members - d) % members
        return pltpu.make_async_remote_copy(
            src_ref=stage.at[r, m],
            dst_ref=got.at[r, m],
            send_sem=s2_send.at[r, d - 1],
            recv_sem=s2_recv.at[r, d - 1],
            device_id=(z * inner + m // ncol, m % ncol),
            device_id_type=MESH,
        )

    fill(0, 0)
    pl.semaphore_wait(barrier, planes + members - 2)

    def first(k, carry):
        fill(k, carry)
        for d in range(1, planes):
            hop1(k - 1, d).start()
        return carry

    lax.fori_loop(1, chunks, first, 0)
    for d in range(1, planes):
        hop1(chunks - 1, d).start()

    def ladder(r):
        for d in range(1, members):
            got_from(r, d).wait_recv()
        for m in range(members):
            for p in range(planes):
                flat[pl.ds((p * members + m) * local * SUB, local * SUB), :] = got[
                    r, m, pl.ds(p * local, local)
                ].reshape(local * SUB, LANES)
        for k in range(SUB):
            a = flat[pl.ds(k, rows, stride=SUB), :]
            high = a.astype(jnp.bfloat16)
            low = (a - high.astype(jnp.float32)).astype(jnp.bfloat16)
            both[pl.ds(0, rows), pl.ds(k * LANES, LANES)] = high
            both[pl.ds(rows, rows), pl.ds(k * LANES, LANES)] = low
        fetch(r).wait()
        dims = (((1,), (1,)), ((), ()))
        step = 256
        for i in range(TB * TB // step):
            part = pl.ds(i * step, step)
            v = vbuf[r % 2, part, :]
            vh = v.astype(jnp.bfloat16)
            vl = (v - vh.astype(jnp.float32)).astype(jnp.bfloat16)
            b = both[...]
            total[part, :] += lax.dot_general(
                vh, b, dims, preferred_element_type=jnp.float32
            ) + lax.dot_general(vl, b, dims, preferred_element_type=jnp.float32)

        @pl.when(r + 2 < slots)
        def _():
            fetch(r + 2).start()

    def ladders(k):
        def one(i, c):
            ladder(k * per_chunk + i)
            return c

        lax.fori_loop(0, per_chunk, one, 0)

    def step(k, carry):
        @pl.when(k < chunks)
        def _():
            for d in range(1, planes):
                source = (z + planes - d) % planes
                hop1(k, d).wait_recv()
                acc[pl.ds(1 + k * ct, ct), pl.ds(source * local, local)] = land[k, d - 1]
            for i in range(per_chunk):
                r = k * per_chunk + i

                def one(m, c):
                    stage[r, m] = acc[relay_ref[r * members + m]]
                    return c

                lax.fori_loop(0, members, one, 0)
            for i in range(per_chunk):
                r = k * per_chunk + i
                got[r, me] = acc[relay_ref[r * members + me]]
            for i in range(per_chunk):
                for d in range(1, members):
                    hop2(k * per_chunk + i, d).start()

        @pl.when(k > 0)
        def _():
            ladders(k - 1)

        return carry

    lax.fori_loop(0, chunks + 1, step, 0)

    def drain1(k, carry):
        for d in range(1, planes):
            hop1(k, d).wait_send()
        return carry

    def drain2(r, carry):
        for d in range(1, members):
            hop2(r, d).wait_send()
        return carry

    lax.fori_loop(0, chunks, drain1, 0)
    lax.fori_loop(0, slots, drain2, 0)
    out_ref[...] = (total[:, :rows] + total[:, rows:]).T


def exchange(planes, inner, ncol, chunks, ct, cap_max, tag, lists, relay, amplitudes, integrals):
    local, wide, _ = amplitudes.shape
    slots, size, _ = integrals.shape
    members = inner * ncol
    nvt = wide // TB
    quads = wide // LANES
    depth = planes * local
    rows = members * depth
    cfg = (planes, inner, ncol, local, slots, chunks, ct, cap_max, nvt)
    f32 = jnp.float32
    return pl.pallas_call(
        functools.partial(exchange_kernel, cfg),
        out_shape=jax.ShapeDtypeStruct((rows, size), f32),
        in_specs=[
            pl.BlockSpec(memory_space=pltpu.SMEM),
            pl.BlockSpec(memory_space=pltpu.SMEM),
            pl.BlockSpec(memory_space=pl.ANY),
            pl.BlockSpec(memory_space=pl.ANY),
        ],
        out_specs=pl.BlockSpec(memory_space=pltpu.VMEM),
        scratch_shapes=[
            pltpu.VMEM((quads * local * wide, LANES), f32),
            pltpu.VMEM((nvt * nvt, local, SUB, LANES), f32),
            pltpu.VMEM((chunks, planes - 1, ct, local, SUB, LANES), f32),
            pltpu.VMEM((chunks, planes - 1, ct, local, SUB, LANES), f32),
            pltpu.VMEM((chunks * ct + 1, depth, SUB, LANES), f32),
            pltpu.VMEM((slots, members, depth, SUB, LANES), f32),
            pltpu.VMEM((slots, members, depth, SUB, LANES), f32),
            pltpu.VMEM((2, size, size), f32),
            pltpu.VMEM((rows * SUB, LANES), f32),
            pltpu.VMEM((2 * rows, size), jnp.bfloat16),
            pltpu.VMEM((size, 2 * rows), f32),
            pltpu.SemaphoreType.DMA((quads * local,)),
            pltpu.SemaphoreType.DMA((chunks, planes - 1)),
            pltpu.SemaphoreType.DMA((chunks, planes - 1)),
            pltpu.SemaphoreType.DMA((slots, members - 1)),
            pltpu.SemaphoreType.DMA((slots, members - 1)),
            pltpu.SemaphoreType.DMA((2,)),
        ],
        compiler_params=pltpu.CompilerParams(
            collective_id=tag, has_side_effects=True, vmem_limit_bytes=63 * 1024 * 1024
        ),
        name="exchange",
    )(lists, relay, amplitudes, integrals)


def tables(task_table, planes, members, z, nvt):
    slots = task_table.shape[1]
    upper, lower = task_table[:, :, 0], task_table[:, :, 1]
    ids = jnp.where(upper >= 0, upper * nvt + lower, -1).reshape(planes, members, slots)
    order = jnp.transpose(ids[:, :, ::-1], (0, 2, 1)).reshape(planes, slots * members)
    valid = (order >= 0).astype(jnp.int32)
    place = jnp.cumsum(valid, axis=1)
    fullest = jnp.max(place[:, -1])
    cap_max = slots * members
    at = jnp.arange(1, cap_max + 1, dtype=jnp.int32)
    hit = (place[:, None, :] == at[None, :, None]) & (valid[:, None, :] > 0)
    lists = jnp.sum(jnp.where(hit, order[:, None, :], 0), axis=2)
    relay = lax.dynamic_index_in_dim(place * valid, z, 0, keepdims=False)
    return lists.reshape(-1), relay, fullest


def body(amplitudes, integrals, coupling, task_table):
    nrow, ncol = lax.axis_size("row"), lax.axis_size("col")
    devices_all = nrow * ncol
    local_rows, wide, _ = amplitudes.shape
    slots = integrals.shape[0]
    total_rows = devices_all * local_rows
    nvt = wide // TB
    inner = 2
    planes = nrow // inner
    members = inner * ncol
    z = lax.axis_index("row") // inner

    first_tile = amplitudes[:, :TB, :]
    pieces = lax.all_to_all(first_tile, ("row", "col"), split_axis=2, concat_axis=0, tiled=True)

    lists, relay, fullest = tables(task_table, planes, members, z, nvt)
    cap_max = slots * members
    mean = nvt * nvt // planes
    chunks = max(slots // 2, 1)
    unit = mean // chunks
    sizes = sorted({unit + -(-unit * n // 8) for n in (1, 2, 3, 4, 6, 8)})
    branches = [
        functools.partial(exchange, planes, inner, ncol, chunks, ct, cap_max, tag)
        for tag, ct in enumerate(sizes)
    ]
    limits = jnp.array([ct * chunks for ct in sizes[:-1]], jnp.int32)
    pick = jnp.sum((fullest > limits).astype(jnp.int32))
    ladder = lax.switch(pick, branches, lists, relay, amplitudes, integrals)

    width_part = pieces.shape[2]
    occupied = coupling.shape[1]
    window = total_rows // occupied
    regrouped = jnp.transpose(
        pieces.reshape(window, occupied, TB, width_part), (0, 2, 3, 1)
    ).reshape(window * TB, width_part * occupied)
    coupling_rows = coupling.reshape(width_part * occupied, occupied * TB)
    hole_term = jnp.dot(
        regrouped,
        coupling_rows,
        precision=lax.Precision.HIGHEST,
        preferred_element_type=jnp.float32,
    )
    hole_term = jnp.transpose(hole_term.reshape(window, TB, occupied, TB), (0, 2, 1, 3)).reshape(
        total_rows, TB * TB
    )
    partial = (ladder + hole_term).reshape(devices_all, local_rows * SUB, LANES)
    shares = lax.all_to_all(partial, ("row", "col"), split_axis=0, concat_axis=0, tiled=True)
    return jnp.sum(shares, axis=0).reshape(local_rows, TB * TB)


def solution(mesh):
    in_specs = (
        P(("row", "col"), None, None),
        P(("row", "col"), None, None),
        P(("row", "col"), None, None),
        P(),
    )
    out_specs = P(("row", "col"), None)
    return jax.shard_map(body, mesh=mesh, in_specs=in_specs, out_specs=out_specs, check_vma=False)
```

time: 285 us -> 206 us (0.72)
  waiting for transfers between devices: 172 us -> 0.01 us
  Pallas kernels: 50.6 us -> 151 us
  starting transfers between devices: 13.3 us -> 7.33 us
  local copies, waits for them, and re-layouts: 14.2 us -> 10 us
  other arithmetic: 2.06 us -> 4.92 us
    all_to_all x1 -> x0, waiting for transfers between devices: 172 us -> none  [body(): lax.all_to_all(outgoing, ('row', 'col'), split_axis=0, concat_axis=0, til...]
    pallas_call x2 -> x1, Pallas kernels: 50.6 us -> 151 us  [exchange(): pl.pallas_call(functools.partial(exchange_kernel, cfg), out_shape=jax.Sha...]
    all_to_all x1 -> x0, starting transfers between devices: 5.96 us -> none  [body(): lax.all_to_all(outgoing, ('row', 'col'), split_axis=0, concat_axis=0, til...]
    unnamed x10, local copies, waits for them, and re-layouts: 7.32 us -> 2.09 us
  transfers between devices with their start and end apart: 2 -> 1, of which waited for: 1 -> 0; matrix products, arithmetic and copies ran while one was open for 5% -> 2% of each run, Pallas kernels for 9% -> 73%
where the time goes in v1:
time: 206 us
  Pallas kernels  151 us (73%)
  blocking collectives  25.1 us (12%)
  local copies, waits for them, and re-layouts  10 us (5%)
  starting transfers between devices  7.33 us (4%)
  matrix products  6.4 us (3%)
  other arithmetic  4.92 us (2%)
    pallas_call x1, Pallas kernels, exchange(): pl.pallas_call(functools.partial(exchange_kernel, cfg), out_shape=jax.Sha...  151 us
    all_to_all x1, blocking collectives, body(): lax.all_to_all(partial, ('row', 'col'), split_axis=0, concat_axis=0, tile...  25.1 us
    all_to_all x1, starting transfers between devices, body(): lax.all_to_all(first_tile, ('row', 'col'), split_axis=2, concat_axis=0, t...  7.33 us
    dot_general x1, matrix products, body(): jnp.dot(regrouped, coupling_rows, precision=lax.Precision.HIGHEST, prefer...  6.4 us
  transfers between devices with their start and end apart: 1, of which 0 were waited for; matrix products, arithmetic and copies ran while one was open for 2% of the time, Pallas kernels for 73%

profile of v1, /device:TPU:0, one launch (start us, length us, event | category | flops | bytes accessed | tf_op | source)
XLA Modules:
  0.0 205.8 jit_solution(784058305257226116)
XLA Ops:
  0.0 1.1 slice.15
  1.1 0.4 copy.26
  1.5 1.4 reshape.61
  2.9 7.3 %all-to-all-start = ((f32[32,1,2048]{2,1,0:T(1,128)}), f32[32,1,2048]{2,1,0:T(1,128)S(1)}, u32[]{:S(2)}, u32[]{:S(2)}) async-start(f32[32,1,2048]{2,1,0:T(1,128)} %reshape.61), calls=%async_computation | async-start | bytes 524288 | tf_op jit(solution)/shard_map/all_to_all | solution.py:311
  10.6 0.1 reshape.51
  10.7 0.3 reduce_window_sum.11
  11.0 0.7 slice_reduce_fusion
  11.7 1.3 fusion.1
  13.0 1.9 copy.30
  15.5 0.2 select_reduce_fusion
  15.7 151.3 %conditional.1 = (f32[128,1024]{1,0:T(8,128)S(1)}) conditional(s32[]{:T(128)} %clamp.3, (s32[512]{0:T(512)S(1)}, s32[128]{0:T(128)S(1)}, f32[4,512,512]{2,1,0:T(8,128)}, f32[16,1024,1024]{2,1,0:T(8,128)}) %tuple.32, (s32[512]{0:T(512)S(1)}, s32[128]{0:T(128)S(1)}, f32[4,512,512]{2,1,0:T(8,128)}, ...), branch_computations={%region_4.5_spmd, %region_5.6_spmd, %region_6.7_spmd, %region_7.8_... | conditional | bytes 8 | solution.py:325
  15.7 151.0 %exchange.7 = f32[128,1024]{1,0:T(8,128)S(1)} custom-call(s32[512]{0:T(512)S(1)} %get-tuple-element.64.list_ref, s32[128]{0:T(128)S(1)} %get-tuple-element.65.relay_ref, f32[4,512,512]{2,1,0:T(8,128)} %get-tuple-element.66.amp_ref, f32[16,1024,1024]{2,1,0:T(8,128)} %get-tuple-element.67.v_ref), custom_call_target="tpu_custom_call" | custom-call | tf_op jit(solution)/shard_map/cond/branch_1_fun/exchange/pallas_call | solution.py:246
  167.0 0.5 broadcast.25
  167.5 1.3 reduce.1
  168.8 0.5 reshape.62
  169.4 0.1 copy.28
  169.6 0.7 copy.29
  170.3 0.4 reshape.58
  170.7 6.4 %convolution_bitcast_fusion = f32[4,32,32,32]{3,2,1,0:T(8,128)S(1)} fusion(f32[32,32,512,1]{2,1,0,3:T(8,128)} %bitcast.30, f32[4,32,512,1]{2,1,0,3:T(8,128)S(1)} %reshape.58), kind=kOutput, calls=%fused_computation | convolution fusion | flops 805306368 | bytes 2883584 | tf_op jit(solution)/shard_map/dot_general | solution.py:334
  177.1 1.7 reshape.55
  178.8 1.1 add.27
  179.9 0.1 reshape.56
  180.0 25.1 %all_to_all.20 = f32[32,32,128]{2,1,0:T(8,128)S(1)} all-to-all(f32[32,32,128]{2,1,0:T(8,128)S(1)} %reshape.56), channel_id=1, replica_groups=mesh['row'=8,'col'=4] {'row','col'}, dimensions={0} | all-to-all | bytes 1048576 | tf_op jit(solution)/shard_map/all_to_all | solution.py:344
  205.2 0.6 reshape.57
  (20 shorter events, 0.5 us)
Async XLA Ops:
  0.0 11.7 %copy-start.2 = (s32[5]{0:T(128)S(1)}, s32[5]{0:T(128)}, u32[]{:S(2)}) copy-start(s32[5]{0:T(128)} %constant.45.clone) | copy-start | bytes 64
  0.0 10.3 %copy-start.1 = (s32[32,16,2]{0,2,1:T(2,128)S(1)}, s32[32,16,2]{0,2,1:T(2,128)}, u32[]{:S(2)}) copy-start(s32[32,16,2]{0,2,1:T(2,128)} %param.14) | copy-start | bytes 12292
  0.0 13.0 %copy-start = (f32[16,32,1024]{2,1,0:T(8,128)S(1)}, f32[16,32,1024]{2,1,0:T(8,128)}, u32[]{:S(2)}) copy-start(f32[16,32,1024]{2,1,0:T(8,128)} %param.13) | copy-start | bytes 6291460
  2.9 164.1 %all-to-all-start = ((f32[32,1,2048]{2,1,0:T(1,128)}), f32[32,1,2048]{2,1,0:T(1,128)S(1)}, u32[]{:S(2)}, u32[]{:S(2)}) async-start(f32[32,1,2048]{2,1,0:T(1,128)} %reshape.61), calls=%async_computation | async-start | bytes 524288 | tf_op jit(solution)/shard_map/all_to_all | solution.py:311
